TPU v7x, 128 devices: a whole 4x4x4 slice. The times are simulated.
128 devices in a mesh: dp: 8 (over z_hi, x), expert: 16 (over y, z_lo, core).
Axes of the slice: x: 4, y: 4, z: 4 (z_hi: 2, z_lo: 2; z = z_hi * 2 + z_lo), core: 2. Of those that a mesh axis runs over, the one named last changes fastest.
Arguments:
- tokens: bfloat16 [32768, 2048], P(('dp', 'expert')), may hold values from -6 to 6
- expert_ids: int32 [32768, 8], P(('dp', 'expert')), may hold values from 0 to 31, all different within a row; in each aligned block of 256 rows (0 to 255, 256 to 511, ...) at most 80 rows name the same one
- route_probs: float32 [32768, 8], P(('dp', 'expert')), may hold values from 0.05 to 1
- w_gate_up: bfloat16 [32, 2048, 1536], P('expert', 'dp'), may hold values from -0.125 to 0.125
- w_down: bfloat16 [32, 768, 2048], P('expert', None, 'dp'), may hold values from -0.21875 to 0.21875
Outputs:
- moe_out: bfloat16 [32768, 2048], P(('dp', 'expert'))
Inputs may be any that keep to these rules, and one draw needn't show every extreme that they name: `expert_ids`: each row names 8 different experts. Among the rows of one device no expert is named more than 80 times, and in every draw some expert is named exactly 80 times in some device's rows.
All inputs are finite; a program needn't handle non-finite values.
Results may differ from a plain program's by a relative error of at most 0.0057.
Values may be sent and summed in bfloat16 or wider, within the bound.
A program may use at most 128 MiB of HBM per device.

v0:
```python
import jax
import jax.numpy as jnp
from jax import lax
from jax.sharding import Mesh
from jax.sharding import PartitionSpec as P

DP = ("dp_0", "dp_1")
DP_EXPERT = ("dp_0", "dp_1", "expert")


def joined_along(pieces, dim):
    pieces = jnp.moveaxis(pieces, 0, dim)
    shape = pieces.shape
    return pieces.reshape(*shape[:dim], shape[dim] * shape[dim + 1], *shape[dim + 2 :])


def gather_in_order(array, axes, sequence):
    pieces = array
    for k in sequence:
        pieces = lax.all_gather(pieces, axes[k])
    done = sequence[::-1]
    back = [done.index(k) for k in range(len(axes))]
    pieces = pieces.transpose(*back, *range(len(axes), pieces.ndim))
    return pieces.reshape(-1, *array.shape)


def whole_of(array, axes, sequence, dim):
    return joined_along(gather_in_order(array, axes, sequence), dim)


def shards(tokens, expert_ids, route_probs, w_gate_up, w_down):
    owners = lax.axis_size("expert")
    local_count = w_gate_up.shape[0]
    experts = owners * local_count
    tok_rows = tokens.shape[0]
    model_width = tokens.shape[1]
    top_count = expert_ids.shape[1]
    capacity = 5 * tok_rows * top_count // (4 * experts)
    hidden_units = w_down.shape[1]
    flat_ids = expert_ids.reshape(-1)
    onehot = (flat_ids[:, None] == jnp.arange(experts, dtype=jnp.int32)[None, :]).astype(jnp.int32)
    before = jnp.cumsum(onehot, axis=0) - onehot
    slot_of = jnp.sum(before * onehot, axis=1)
    target = flat_ids * capacity + slot_of
    copies = jnp.repeat(tokens, top_count, axis=0)
    send_buffer = jnp.zeros((experts * capacity, model_width), jnp.bfloat16).at[target].set(copies)
    send_buffer = send_buffer.reshape(experts, capacity, model_width)
    received = lax.all_to_all(send_buffer, "expert", split_axis=0, concat_axis=1, tiled=True)
    returned_list = []
    for local_expert in range(local_count):
        rows_in = received[local_expert]
        joined = jnp.dot(
            rows_in,
            whole_of(w_gate_up[local_expert], DP, (0, 1), 0),
            preferred_element_type=jnp.float32,
        )
        hidden = (jax.nn.silu(joined[:, :hidden_units]) * joined[:, hidden_units:]).astype(
            jnp.bfloat16
        )
        returned_list.append(
            lax.all_to_all(
                jnp.dot(
                    hidden,
                    lax.all_gather(w_down[local_expert], DP, axis=1, tiled=True),
                    preferred_element_type=jnp.float32,
                ).astype(jnp.bfloat16),
                "expert",
                split_axis=0,
                concat_axis=0,
                tiled=True,
            )
        )
    returned = jnp.concatenate(returned_list, axis=0)
    source_rows = (
        flat_ids % local_count * (owners * capacity) + flat_ids // local_count * capacity + slot_of
    )
    gathered = returned[source_rows].reshape(tok_rows, top_count, model_width)
    weights = route_probs / jnp.sum(route_probs, axis=1, keepdims=True)
    combined = jnp.sum(gathered.astype(jnp.float32) * weights[:, :, None], axis=1)
    return combined.astype(jnp.bfloat16)


def solution(mesh):
    finer = Mesh(mesh.devices.reshape(2, 4, mesh.shape["expert"]), ("dp_0", "dp_1", "expert"))
    in_specs = (
        P(DP_EXPERT, None),
        P(DP_EXPERT, None),
        P(DP_EXPERT, None),
        P("expert", DP, None),
        P("expert", None, DP),
    )
    out_specs = P(DP_EXPERT, None)
    return jax.shard_map(
        shards, mesh=finer, in_specs=in_specs, out_specs=out_specs, check_vma=False
    )
```

profile of v0, /device:TPU:49, one launch (start us, length us, event | category | flops | bytes accessed | tf_op | source)
XLA Modules:
  0.0 568.1 jit_solution(15967926868259111235)
XLA Ops:
  6.5 2.8 fusion.23
  9.3 0.0 all-gather.11.cloned.1.call-update
  9.3 0.0 all-gather.13.cloned.1.call-start
  9.4 0.7 all-gather.13.cloned.1.call-update
  10.1 0.0 all-gather.15.cloned.1.call-start
  10.1 31.5 %all-gather.11.cloned.1.call-done = bf16[2,256,1536]{2,1,0:T(8,128)(2,1)} async-done(((bf16[1,256,1536]{2,1,0:T(8,128)(2,1)}), bf16[2,256,1536]{2,1,0:T(8,128)(2,1)}) %all-gather.11.cloned.1.call-update) | async-done | bytes 1572880 | tf_op jit(solution)/shard_map/all_gather | solution.py:20
  41.6 0.0 all-gather.15.cloned.1.call-update
  41.6 0.0 all-gather.17.cloned.1.call-start
  41.7 1.0 fusion.24
  42.7 0.0 all-gather.17.cloned.1.call-update
  42.7 0.1 copy.21
  42.8 0.1 eq.31
  42.9 0.1 eq.27
  43.0 0.1 reshape.185
  43.2 9.1 %reduce-window.6 = s32[32,16,128]{2,1,0:T(8,128)S(1)} reduce-window(s32[32,16,128]{2,1,0:T(8,128)S(1)} %fusion.16, s32[]{:T(128)} %constant.38.clone.1), window={size=1x1x128 pad=0_0x0_0x127_0}, to_apply=%region_0.0 | reduce-window | flops 8323072 | bytes 524292 | tf_op jit(solution)/shard_map/reduce-window
  52.3 0.1 slice.52
  52.4 0.2 copy.29
  52.7 0.2 reduce-window.9
  52.8 0.1 broadcast_add_fusion
  53.0 0.1 fusion.15
  53.1 0.1 compare_select_fusion
  53.2 17.9 %scatter_custom_fusion = bf16[2560,2048]{1,0:T(8,128)(2,1)} fusion(s32[2048]{0:T(1024)S(1)} %bitcast.73, bf16[]{:T(256)} %constant.36.clone.1, bf16[256,2048]{1,0:T(8,128)(2,1)S(1)} %copy-done), kind=kCustom, calls=%fused_computation.5 | custom fusion | bytes 11534338 | tf_op jit(solution)/shard_map/scatter | solution.py:46
  71.1 6.4 %all-to-all-start = ((bf16[32,80,2048]{2,1,0:T(8,128)(2,1)}), bf16[32,80,2048]{2,1,0:T(8,128)(2,1)}, u32[]{:S(2)}, u32[]{:S(2)}) async-start(bf16[32,80,2048]{2,1,0:T(8,128)(2,1)} %bitcast.57), calls=%async_computation | async-start | bytes 20971520 | tf_op jit(solution)/shard_map/all_to_all | solution.py:48
  77.5 0.0 all-gather.19.cloned.1.call-start
  77.6 0.0 all-gather.13.cloned.1.call-done
  77.6 0.5 all-gather.19.cloned.1.call-update
  78.1 0.5 all-gather.21.cloned.1.call-start
  78.6 0.1 all-gather.21.cloned.1.call-update
  78.7 165.6 %all-to-all-done = bf16[32,80,2048]{2,1,0:T(8,128)(2,1)} async-done(((bf16[32,80,2048]{2,1,0:T(8,128)(2,1)}), bf16[32,80,2048]{2,1,0:T(8,128)(2,1)}, u32[]{:S(2)}, u32[]{:S(2)}) %all-to-all-start) | async-done | bytes 10485792 | tf_op jit(solution)/shard_map/all_to_all | solution.py:48
  244.3 10.1 %fusion.22 = (bf16[1,16,80,2048]{3,2,0,1:T(8,128)(2,1)}, bf16[1,16,80,2048]{3,2,0,1:T(8,128)(2,1)}) fusion(bf16[2,16,80,2048]{3,2,0,1:T(8,128)(2,1)} %bitcast.8), kind=kLoop, calls=%fused_computation.41 | loop fusion | bytes 20971520 | tf_op jit(solution)/shard_map/slice | solution.py:51
  254.4 3.6 copy.26
  258.0 0.7 copy-done.2
  258.7 10.6 %fusion.25 = f32[1280,1536]{1,0:T(8,128)} fusion(bf16[1280,2048]{1,0:T(8,128)(2,1)S(1)} %bitcast.65, bf16[2048,1536]{1,0:T(8,128)(2,1)S(1)} %bitcast.61), kind=kOutput, calls=%fused_computation.44 | convolution fusion | flops 8053063680 | bytes 19398656 | tf_op jit(solution)/shard_map/dot_general | solution.py:52
  269.3 10.9 %convolution_convert_fusion.1 = bf16[1280,2048]{1,0:T(8,128)(2,1)} fusion(bf16[1,768,2048]{2,1,0:T(8,128)(2,1)} %all-gather.17.cloned.1.call-done, f32[1280,1536]{1,0:T(8,128)} %fusion.25), kind=kOutput, calls=%fused_computation.8 | convolution fusion | flops 4035051520 | bytes 16252928 | tf_op jit(solution)/shard_map/dot_general | solution.py:62
  280.2 9.1 %all-to-all-start.1 = ((bf16[16,80,2048]{2,1,0:T(8,128)(2,1)}), bf16[16,80,2048]{2,1,0:T(8,128)(2,1)}, u32[]{:S(2)}, u32[]{:S(2)}) async-start(bf16[16,80,2048]{2,1,0:T(8,128)(2,1)} %bitcast.66), calls=%async_computation.1 | async-start | bytes 10485760 | tf_op jit(solution)/shard_map/all_to_all | solution.py:61
  289.3 48.6 %all-gather.19.cloned.1.call-done = bf16[8,256,1536]{2,1,0:T(8,128)(2,1)} async-done(((bf16[2,256,1536]{2,1,0:T(8,128)(2,1)}), bf16[8,256,1536]{2,1,0:T(8,128)(2,1)}) %all-gather.19.cloned.1.call-update) | async-done | bytes 6291472 | tf_op jit(solution)/shard_map/all_gather | solution.py:20
  337.9 3.6 copy.27
  341.6 0.4 slice-done.1
  341.9 10.5 %fusion.26 = f32[1280,1536]{1,0:T(8,128)} fusion(bf16[1280,2048]{1,0:T(8,128)(2,1)S(1)} %bitcast.64, bf16[2048,1536]{1,0:T(8,128)(2,1)S(1)} %bitcast.60), kind=kOutput, calls=%fused_computation.45 | convolution fusion | flops 8053063680 | bytes 19398656 | tf_op jit(solution)/shard_map/dot_general | solution.py:52
  352.5 63.8 %all-gather.21.cloned.1.call-done = bf16[1,768,2048]{2,1,0:T(8,128)(2,1)} async-done(((bf16[1,768,256]{2,1,0:T(8,128)(2,1)}), bf16[1,768,2048]{2,1,0:T(8,128)(2,1)}) %all-gather.21.cloned.1.call-update) | async-done | bytes 3145744 | tf_op jit(solution)/shard_map/all_gather | solution.py:64
  416.2 10.8 %convolution_convert_fusion = bf16[1280,2048]{1,0:T(8,128)(2,1)} fusion(bf16[1,768,2048]{2,1,0:T(8,128)(2,1)} %all-gather.21.cloned.1.call-done, f32[1280,1536]{1,0:T(8,128)} %fusion.26), kind=kOutput, calls=%fused_computation.7 | convolution fusion | flops 4035051520 | bytes 16252928 | tf_op jit(solution)/shard_map/dot_general | solution.py:62
  427.0 0.0 all-to-all-done.1
  427.0 7.5 %all-to-all-start.2 = ((bf16[16,80,2048]{2,1,0:T(8,128)(2,1)}), bf16[16,80,2048]{2,1,0:T(8,128)(2,1)}, u32[]{:S(2)}, u32[]{:S(2)}) async-start(bf16[16,80,2048]{2,1,0:T(8,128)(2,1)} %bitcast.67), calls=%async_computation.2 | async-start | bytes 10485760 | tf_op jit(solution)/shard_map/all_to_all | solution.py:61
  434.6 0.1 copy.28
  434.7 79.5 %all-to-all-done.2 = bf16[16,80,2048]{2,1,0:T(8,128)(2,1)} async-done(((bf16[16,80,2048]{2,1,0:T(8,128)(2,1)}), bf16[16,80,2048]{2,1,0:T(8,128)(2,1)}, u32[]{:S(2)}, u32[]{:S(2)}) %all-to-all-start.2) | async-done | bytes 5242912 | tf_op jit(solution)/shard_map/all_to_all | solution.py:61
  514.2 12.7 %pad_maximum_fusion = bf16[2560,2048]{1,0:T(8,128)(2,1)} fusion(bf16[1280,2048]{1,0:T(8,128)(2,1)} %bitcast.23, bf16[1280,2048]{1,0:T(8,128)(2,1)} %bitcast.15), kind=kLoop, calls=%fused_computation.4 | loop fusion | flops 20971520 | bytes 20971520 | tf_op jit(solution)/shard_map/concatenate | solution.py:73
  526.9 21.9 %gather_fusion = bf16[2048,2048]{1,0:T(8,128)(2,1)} fusion(bf16[2560,2048]{1,0:T(8,128)(2,1)} %pad_maximum_fusion, s32[2048]{0:T(1024)S(1)} %broadcast_clamp_fusion), kind=kCustom, calls=%fused_computation | custom fusion | bytes 16785408 | tf_op jit(solution)/shard_map/gather | solution.py:77
  548.8 12.2 %fusion = bf16[256,2048]{1,0:T(8,128)(2,1)} fusion(bf16[2048,2048]{1,0:T(8,128)(2,1)} %gather_fusion, f32[256,8]{1,0:T(8,128)S(1)} %copy.28), kind=kLoop, calls=%fused_computation.3 | loop fusion | flops 12058624 | bytes 9445376 | tf_op jit(solution)/shard_map/reduce_sum | solution.py:79
  (22 shorter events, 0.1 us)
Async XLA Ops:
  6.5 46.7 %copy-start = (bf16[256,2048]{1,0:T(8,128)(2,1)S(1)}, bf16[256,2048]{1,0:T(8,128)(2,1)}, u32[]{:S(2)}) copy-start(bf16[256,2048]{1,0:T(8,128)(2,1)} %param.5) | copy-start | bytes 3145732
  6.5 35.2 %copy-start.3 = (bf16[2,768,256]{2,1,0:T(8,128)(2,1)S(1)}, bf16[2,768,256]{2,1,0:T(8,128)(2,1)}, u32[]{:S(2)}) copy-start(bf16[2,768,256]{2,1,0:T(8,128)(2,1)} %param.9) | copy-start | bytes 2359300
  6.5 36.1 %copy-start.5 = (s32[256,8]{0,1:T(8,128)S(1)}, s32[256,8]{0,1:T(8,128)}, u32[]{:S(2)}) copy-start(s32[256,8]{0,1:T(8,128)} %param.6) | copy-start | bytes 24580
  6.5 35.1 %all-gather.11.cloned.1.call-start = ((), (), s32[]{:S(2)}) async-start(), calls=%async_computation.3 | async-start | bytes 2359296 | tf_op jit(solution)/shard_map/all_gather | solution.py:20
  9.3 68.3 %all-gather.13.cloned.1.call-start = ((), (), s32[]{:S(2)}) async-start(), calls=%async_computation.4 | async-start | bytes 2359296 | tf_op jit(solution)/shard_map/all_gather | solution.py:20
  10.1 244.3 %all-gather.15.cloned.1.call-start = ((), (), s32[]{:S(2)}) async-start(), calls=%async_computation.5 | async-start | bytes 7864320 | tf_op jit(solution)/shard_map/all_gather | solution.py:20
  41.6 227.7 %all-gather.17.cloned.1.call-start = ((), (), s32[]{:S(2)}) async-start(), calls=%async_computation.6 | async-start | bytes 3538944 | tf_op jit(solution)/shard_map/all_gather | solution.py:64
  71.1 173.2 %all-to-all-start = ((bf16[32,80,2048]{2,1,0:T(8,128)(2,1)}), bf16[32,80,2048]{2,1,0:T(8,128)(2,1)}, u32[]{:S(2)}, u32[]{:S(2)}) async-start(bf16[32,80,2048]{2,1,0:T(8,128)(2,1)} %bitcast.57), calls=%async_computation | async-start | bytes 20971520 | tf_op jit(solution)/shard_map/all_to_all | solution.py:48
  77.5 260.4 %all-gather.19.cloned.1.call-start = ((), (), s32[]{:S(2)}) async-start(), calls=%async_computation.7 | async-start | bytes 7864320 | tf_op jit(solution)/shard_map/all_gather | solution.py:20
  78.1 338.1 %all-gather.21.cloned.1.call-start = ((), (), s32[]{:S(2)}) async-start(), calls=%async_computation.8 | async-start | bytes 3538944 | tf_op jit(solution)/shard_map/all_gather | solution.py:64
  254.4 4.3 copy-start.2
  280.2 61.3 %slice-start = ((s8[5242880]{0:T(1024)(128)(4,1)}), s8[1048576]{0:T(1024)(128)(4,1)S(1)}, s32[]{:S(2)}) async-start(s8[5242880]{0:T(1024)(128)(4,1)} %bitcast.62), calls=%async_computation.9 | async-start | bytes 2097152
  280.2 146.8 %all-to-all-start.1 = ((bf16[16,80,2048]{2,1,0:T(8,128)(2,1)}), bf16[16,80,2048]{2,1,0:T(8,128)(2,1)}, u32[]{:S(2)}, u32[]{:S(2)}) async-start(bf16[16,80,2048]{2,1,0:T(8,128)(2,1)} %bitcast.66), calls=%async_computation.1 | async-start | bytes 10485760 | tf_op jit(solution)/shard_map/all_to_all | solution.py:61
  337.9 4.0 slice-start.1
  427.0 7.5 %copy-start.4 = (f32[256,8]{0,1:T(8,128)S(1)}, f32[256,8]{0,1:T(8,128)}, u32[]{:S(2)}) copy-start(f32[256,8]{0,1:T(8,128)} %param.7) | copy-start | bytes 24580
  427.0 87.1 %all-to-all-start.2 = ((bf16[16,80,2048]{2,1,0:T(8,128)(2,1)}), bf16[16,80,2048]{2,1,0:T(8,128)(2,1)}, u32[]{:S(2)}, u32[]{:S(2)}) async-start(bf16[16,80,2048]{2,1,0:T(8,128)(2,1)} %bitcast.67), calls=%async_computation.2 | async-start | bytes 10485760 | tf_op jit(solution)/shard_map/all_to_all | solution.py:61
  526.9 34.2 %copy-start.1 = (bf16[256,2048]{1,0:T(8,128)(2,1)S(1)}, bf16[256,2048]{1,0:T(8,128)(2,1)}, u32[]{:S(2)}) copy-start(bf16[256,2048]{1,0:T(8,128)(2,1)} %param.5) | copy-start | bytes 3145732
Sparse Core Ops, SparseCore 0:
  9.4 32.1 all-gather.10
  43.3 30.5 all-gather.12
  75.5 65.7 all-gather.14
  143.3 99.1 all-gather.16
  244.0 93.8 all-gather.18
  340.0 76.2 all-gather.20
where the time goes:
time: 576 us; the launch traced here: 568 us
  waiting for transfers between devices  390 us (68%)
  local copies, waits for them, and re-layouts  62.9 us (11%)
  matrix products  42.8 us (7%)
  other arithmetic  34.6 us (6%)
  starting transfers between devices  23.7 us (4%)
  between operations  13.9 us (2%)
    all_to_all x1, waiting for transfers between devices, shards(): lax.all_to_all(send_buffer, 'expert', split_axis=0, concat_axis=1, tiled=...  166 us
    all_gather x4, waiting for transfers between devices, gather_in_order(): pieces = lax.all_gather(pieces, axes[k])  80.1 us
    all_to_all x2, waiting for transfers between devices, shards(): lax.all_to_all(jnp.dot(hidden, lax.all_gather(w_down[local_expert], DP, a...  79.5 us
    all_gather x2, waiting for transfers between devices, shards(): lax.all_gather(w_down[local_expert], DP, axis=1, tiled=True)  63.8 us
    gather x1, local copies, waits for them, and re-layouts, shards(): gathered = returned[source_rows].reshape(tok_rows, top_count, model_width)  21.9 us
    dot_general x2, matrix products, shards(): jnp.dot(hidden, lax.all_gather(w_down[local_expert], DP, axis=1, tiled=Tr...  21.7 us
    dot_general x2, matrix products, shards(): jnp.dot(rows_in, whole_of(w_gate_up[local_expert], DP, (0, 1), 0), prefer...  21.1 us
    scatter x1, local copies, waits for them, and re-layouts, shards(): jnp.zeros((experts * capacity, model_width), jnp.bfloat16).at[target]  17.9 us
  transfers between devices with their start and end apart: 9, of which 5 were waited for; matrix products, arithmetic and copies ran while one was open for 16% of the time, Pallas kernels for 0%

commit v1 on v0

--- a/solution.py
+++ b/solution.py
@@ -57,11 +57,23 @@
         hidden = (jax.nn.silu(joined[:, :hidden_units]) * joined[:, hidden_units:]).astype(
             jnp.bfloat16
         )
+
+        def recover_object_for(xx, row_axis):
+            return jnp.concatenate(
+                lax.all_to_all(
+                    jnp.stack([xx for _ in range(lax.axis_size(row_axis))]),
+                    axis_name=row_axis,
+                    split_axis=0,
+                    concat_axis=0,
+                ),
+                axis=1,
+            )
+
         returned_list.append(
             lax.all_to_all(
                 jnp.dot(
                     hidden,
-                    lax.all_gather(w_down[local_expert], DP, axis=1, tiled=True),
+                    recover_object_for(w_down[local_expert], DP),
                     preferred_element_type=jnp.float32,
                 ).astype(jnp.bfloat16),
                 "expert",

time: 576 us -> 594 us (1.031)
  the two profiles are of different devices: /device:TPU:49 before, /device:TPU:119 now
where the time goes in v1:
time: 594 us; the launch traced here: 586 us
  waiting for transfers between devices  389 us (65%)
  local copies, waits for them, and re-layouts  67.7 us (11%)
  matrix products  41.4 us (7%)
  starting transfers between devices  39.4 us (7%)
  other arithmetic  34.6 us (6%)
  between operations  13.6 us (2%)
    all_to_all x1, waiting for transfers between devices, shards(): lax.all_to_all(send_buffer, 'expert', split_axis=0, concat_axis=1, tiled=...  170 us
    all_to_all x2, waiting for transfers between devices, shards(): lax.all_to_all(jnp.dot(hidden, recover_object_for(w_down[local_expert], D...  135 us
    all_to_all x2, waiting for transfers between devices, recover_object_for(): lax.all_to_all(jnp.stack([xx for _ in range(lax.axis_size(row_axis))]), a...  53.2 us
    all_gather x4, waiting for transfers between devices, gather_in_order(): pieces = lax.all_gather(pieces, axes[k])  29.8 us
    dot_general x2, matrix products, shards(): jnp.dot(rows_in, whole_of(w_gate_up[local_expert], DP, (0, 1), 0), prefer...  22.6 us
    gather x1, local copies, waits for them, and re-layouts, shards(): gathered = returned[source_rows].reshape(tok_rows, top_count, model_width)  21.9 us
    all_to_all x2, starting transfers between devices, recover_object_for(): lax.all_to_all(jnp.stack([xx for _ in range(lax.axis_size(row_axis))]), a...  19.4 us
    dot_general x2, matrix products, shards(): jnp.dot(hidden, recover_object_for(w_down[local_expert], DP), preferred_e...  18.8 us
  transfers between devices with their start and end apart: 9, of which 6 were waited for; matrix products, arithmetic and copies ran while one was open for 16% of the time, Pallas kernels for 0%

profile of v1, /device:TPU:119, one launch (start us, length us, event | category | flops | bytes accessed | tf_op | source)
XLA Modules:
  0.0 585.6 jit_solution(609043987441414186)
XLA Ops:
  6.5 2.7 fusion.21
  9.3 0.0 all-gather.9.cloned.1.call-start
  9.3 0.7 all-gather.9.cloned.1.call-update
  10.0 0.0 all-gather.11.cloned.1.call-start
  10.1 29.7 %all-gather.7.cloned.1.call-done = bf16[2,256,1536]{2,1,0:T(8,128)(2,1)} async-done(((bf16[1,256,1536]{2,1,0:T(8,128)(2,1)}), bf16[2,256,1536]{2,1,0:T(8,128)(2,1)}) %all-gather.7.cloned.1.call-update) | async-done | bytes 1572880 | tf_op jit(solution)/shard_map/all_gather | solution.py:20
  39.9 0.1 copy.25
  40.0 0.1 eq.31
  40.1 0.1 eq.27
  40.2 0.1 reshape.199
  40.4 9.1 %reduce-window.6 = s32[32,16,128]{2,1,0:T(8,128)S(1)} reduce-window(s32[32,16,128]{2,1,0:T(8,128)S(1)} %fusion.14, s32[]{:T(128)} %constant.38.clone.1), window={size=1x1x128 pad=0_0x0_0x127_0}, to_apply=%region_0.0 | reduce-window | flops 8323072 | bytes 524292 | tf_op jit(solution)/shard_map/reduce-window
  49.4 0.1 slice.58
  49.6 0.2 copy.35
  49.8 0.2 reduce-window.9
  50.0 0.1 broadcast_add_fusion
  50.2 0.1 fusion.13
  50.3 0.1 compare_select_fusion
  50.4 17.9 %scatter_custom_fusion = bf16[2560,2048]{1,0:T(8,128)(2,1)} fusion(s32[2048]{0:T(1024)S(1)} %bitcast.79, bf16[]{:T(256)} %constant.36.clone.1, bf16[256,2048]{1,0:T(8,128)(2,1)S(1)} %copy-done), kind=kCustom, calls=%fused_computation.5 | custom fusion | bytes 11534338 | tf_op jit(solution)/shard_map/scatter | solution.py:46
  68.3 6.3 %all-to-all-start = ((bf16[32,80,2048]{2,1,0:T(8,128)(2,1)}), bf16[32,80,2048]{2,1,0:T(8,128)(2,1)}, u32[]{:S(2)}, u32[]{:S(2)}) async-start(bf16[32,80,2048]{2,1,0:T(8,128)(2,1)} %bitcast.63), calls=%async_computation | async-start | bytes 20971520 | tf_op jit(solution)/shard_map/all_to_all | solution.py:48
  74.6 0.0 all-gather.13.cloned.1.call-start
  74.6 0.0 all-gather.9.cloned.1.call-done
  74.6 0.5 all-gather.13.cloned.1.call-update
  75.2 0.1 slice_bitcast_fusion.1
  75.2 0.2 copy.31
  75.4 169.7 %all-to-all-done = bf16[32,80,2048]{2,1,0:T(8,128)(2,1)} async-done(((bf16[32,80,2048]{2,1,0:T(8,128)(2,1)}), bf16[32,80,2048]{2,1,0:T(8,128)(2,1)}, u32[]{:S(2)}, u32[]{:S(2)}) %all-to-all-start) | async-done | bytes 10485792 | tf_op jit(solution)/shard_map/all_to_all | solution.py:48
  245.1 1.8 stack.6
  247.0 13.1 %all-to-all-start.1 = ((bf16[8,768,256]{1,2,0:T(8,128)(2,1)}), bf16[8,768,256]{1,2,0:T(8,128)(2,1)}, u32[]{:S(2)}, u32[]{:S(2)}) async-start(bf16[8,768,256]{1,2,0:T(8,128)(2,1)} %stack.6), calls=%async_computation.1 | async-start | bytes 6291456 | tf_op jit(solution)/shard_map/all_to_all | solution.py:63
  260.0 0.2 copy.33
  260.2 10.2 %fusion.20 = (bf16[1,16,80,2048]{3,2,0,1:T(8,128)(2,1)}, bf16[1,16,80,2048]{3,2,0,1:T(8,128)(2,1)}) fusion(bf16[2,16,80,2048]{3,2,0,1:T(8,128)(2,1)} %bitcast.8), kind=kLoop, calls=%fused_computation.41 | loop fusion | bytes 20971520 | tf_op jit(solution)/shard_map/slice | solution.py:51
  270.4 5.8 copy.30
  276.3 30.4 %all-to-all-done.1 = bf16[8,768,256]{1,2,0:T(8,128)(2,1)} async-done(((bf16[8,768,256]{1,2,0:T(8,128)(2,1)}), bf16[8,768,256]{1,2,0:T(8,128)(2,1)}, u32[]{:S(2)}, u32[]{:S(2)}) %all-to-all-start.1) | async-done | bytes 3145760 | tf_op jit(solution)/shard_map/all_to_all | solution.py:63
  306.6 1.9 stack.7
  308.5 6.4 %all-to-all-start.3 = ((bf16[8,768,256]{1,2,0:T(8,128)(2,1)}), bf16[8,768,256]{1,2,0:T(8,128)(2,1)}, u32[]{:S(2)}, u32[]{:S(2)}) async-start(bf16[8,768,256]{1,2,0:T(8,128)(2,1)} %stack.7), calls=%async_computation.3 | async-start | bytes 6291456 | tf_op jit(solution)/shard_map/all_to_all | solution.py:63
  314.9 12.1 %fusion.22 = f32[1280,1536]{1,0:T(8,128)S(1)} fusion(bf16[1280,2048]{1,0:T(8,128)(2,1)} %bitcast.71, bf16[2048,1536]{1,0:T(8,128)(2,1)} %bitcast.66), kind=kOutput, calls=%fused_computation.43 | convolution fusion | flops 8053063680 | bytes 19398656 | tf_op jit(solution)/shard_map/dot_general | solution.py:52
  327.0 8.0 %convolution_convert_fusion.1 = bf16[1280,2048]{1,0:T(8,128)(2,1)} fusion(bf16[768,2048]{0,1:T(8,128)(2,1)} %bitcast.15, f32[1280,1536]{1,0:T(8,128)S(1)} %fusion.22), kind=kOutput, calls=%fused_computation.8 | convolution fusion | flops 4035051520 | bytes 16252928 | tf_op jit(solution)/shard_map/dot_general | solution.py:74
  334.9 22.8 %all-to-all-done.3 = bf16[8,768,256]{1,2,0:T(8,128)(2,1)} async-done(((bf16[8,768,256]{1,2,0:T(8,128)(2,1)}), bf16[8,768,256]{1,2,0:T(8,128)(2,1)}, u32[]{:S(2)}, u32[]{:S(2)}) %all-to-all-start.3) | async-done | bytes 3145760 | tf_op jit(solution)/shard_map/all_to_all | solution.py:63
  357.8 8.0 %all-to-all-start.2 = ((bf16[16,80,2048]{2,1,0:T(8,128)(2,1)}), bf16[16,80,2048]{2,1,0:T(8,128)(2,1)}, u32[]{:S(2)}, u32[]{:S(2)}) async-start(bf16[16,80,2048]{2,1,0:T(8,128)(2,1)} %bitcast.72), calls=%async_computation.2 | async-start | bytes 10485760 | tf_op jit(solution)/shard_map/all_to_all | solution.py:73
  365.7 0.0 all-gather.13.cloned.1.call-done
  365.8 3.6 copy.32
  369.4 0.4 slice-done.1
  369.8 10.6 %fusion.23 = f32[1280,1536]{1,0:T(8,128)} fusion(bf16[1280,2048]{1,0:T(8,128)(2,1)S(1)} %bitcast.70, bf16[2048,1536]{1,0:T(8,128)(2,1)S(1)} %bitcast.67), kind=kOutput, calls=%fused_computation.44 | convolution fusion | flops 8053063680 | bytes 19398656 | tf_op jit(solution)/shard_map/dot_general | solution.py:52
  380.3 10.9 %convolution_convert_fusion = bf16[1280,2048]{1,0:T(8,128)(2,1)} fusion(bf16[768,2048]{0,1:T(8,128)(2,1)} %bitcast.25, f32[1280,1536]{1,0:T(8,128)} %fusion.23), kind=kOutput, calls=%fused_computation.7 | convolution fusion | flops 4035051520 | bytes 16252928 | tf_op jit(solution)/shard_map/dot_general | solution.py:74
  391.2 54.7 %all-to-all-done.2 = bf16[16,80,2048]{2,1,0:T(8,128)(2,1)} async-done(((bf16[16,80,2048]{2,1,0:T(8,128)(2,1)}), bf16[16,80,2048]{2,1,0:T(8,128)(2,1)}, u32[]{:S(2)}, u32[]{:S(2)}) %all-to-all-start.2) | async-done | bytes 5242912 | tf_op jit(solution)/shard_map/all_to_all | solution.py:73
  445.9 5.6 all-to-all-start.4
  451.5 0.1 copy.34
  451.6 80.4 %all-to-all-done.4 = bf16[16,80,2048]{2,1,0:T(8,128)(2,1)} async-done(((bf16[16,80,2048]{2,1,0:T(8,128)(2,1)}), bf16[16,80,2048]{2,1,0:T(8,128)(2,1)}, u32[]{:S(2)}, u32[]{:S(2)}) %all-to-all-start.4) | async-done | bytes 5242912 | tf_op jit(solution)/shard_map/all_to_all | solution.py:73
  532.0 12.7 %pad_maximum_fusion = bf16[2560,2048]{1,0:T(8,128)(2,1)} fusion(bf16[1280,2048]{1,0:T(8,128)(2,1)} %bitcast.27, bf16[1280,2048]{1,0:T(8,128)(2,1)} %bitcast.17), kind=kLoop, calls=%fused_computation.4 | loop fusion | flops 20971520 | bytes 20971520 | tf_op jit(solution)/shard_map/concatenate | solution.py:85
  544.7 21.9 %gather_fusion = bf16[2048,2048]{1,0:T(8,128)(2,1)} fusion(bf16[2560,2048]{1,0:T(8,128)(2,1)} %pad_maximum_fusion, s32[2048]{0:T(1024)S(1)} %broadcast_clamp_fusion), kind=kCustom, calls=%fused_computation | custom fusion | bytes 16785408 | tf_op jit(solution)/shard_map/gather | solution.py:89
  566.6 12.2 %fusion = bf16[256,2048]{1,0:T(8,128)(2,1)} fusion(bf16[2048,2048]{1,0:T(8,128)(2,1)} %gather_fusion, f32[256,8]{1,0:T(8,128)S(1)} %copy.34), kind=kLoop, calls=%fused_computation.3 | loop fusion | flops 12058624 | bytes 9445376 | tf_op jit(solution)/shard_map/reduce_sum | solution.py:91
  (22 shorter events, 0.1 us)
Async XLA Ops:
  6.5 43.8 %copy-start = (bf16[256,2048]{1,0:T(8,128)(2,1)S(1)}, bf16[256,2048]{1,0:T(8,128)(2,1)}, u32[]{:S(2)}) copy-start(bf16[256,2048]{1,0:T(8,128)(2,1)} %param.5) | copy-start | bytes 3145732
  6.5 33.3 %copy-start.4 = (s32[256,8]{0,1:T(8,128)S(1)}, s32[256,8]{0,1:T(8,128)}, u32[]{:S(2)}) copy-start(s32[256,8]{0,1:T(8,128)} %param.6) | copy-start | bytes 24580
  6.5 33.3 %all-gather.7.cloned.1.call-start = ((), (), s32[]{:S(2)}) async-start(), calls=%async_computation.5 | async-start | bytes 2359296 | tf_op jit(solution)/shard_map/all_gather | solution.py:20
  9.3 65.3 %all-gather.9.cloned.1.call-start = ((), (), s32[]{:S(2)}) async-start(), calls=%async_computation.6 | async-start | bytes 2359296 | tf_op jit(solution)/shard_map/all_gather | solution.py:20
  10.0 260.4 %all-gather.11.cloned.1.call-start = ((), (), s32[]{:S(2)}) async-start(), calls=%async_computation.7 | async-start | bytes 7864320 | tf_op jit(solution)/shard_map/all_gather | solution.py:20
  68.3 6.9 %copy-start.2 = (bf16[2,768,256]{2,1,0:T(8,128)(2,1)S(1)}, bf16[2,768,256]{2,1,0:T(8,128)(2,1)}, u32[]{:S(2)}) copy-start(bf16[2,768,256]{2,1,0:T(8,128)(2,1)} %param.9) | copy-start | bytes 2359300
  68.3 176.8 %all-to-all-start = ((bf16[32,80,2048]{2,1,0:T(8,128)(2,1)}), bf16[32,80,2048]{2,1,0:T(8,128)(2,1)}, u32[]{:S(2)}, u32[]{:S(2)}) async-start(bf16[32,80,2048]{2,1,0:T(8,128)(2,1)} %bitcast.63), calls=%async_computation | async-start | bytes 20971520 | tf_op jit(solution)/shard_map/all_to_all | solution.py:48
  74.6 291.2 %all-gather.13.cloned.1.call-start = ((), (), s32[]{:S(2)}) async-start(), calls=%async_computation.8 | async-start | bytes 7864320 | tf_op jit(solution)/shard_map/all_gather | solution.py:20
  247.0 59.7 %all-to-all-start.1 = ((bf16[8,768,256]{1,2,0:T(8,128)(2,1)}), bf16[8,768,256]{1,2,0:T(8,128)(2,1)}, u32[]{:S(2)}, u32[]{:S(2)}) async-start(bf16[8,768,256]{1,2,0:T(8,128)(2,1)} %stack.6), calls=%async_computation.1 | async-start | bytes 6291456 | tf_op jit(solution)/shard_map/all_to_all | solution.py:63
  308.5 49.2 %all-to-all-start.3 = ((bf16[8,768,256]{1,2,0:T(8,128)(2,1)}), bf16[8,768,256]{1,2,0:T(8,128)(2,1)}, u32[]{:S(2)}, u32[]{:S(2)}) async-start(bf16[8,768,256]{1,2,0:T(8,128)(2,1)} %stack.7), calls=%async_computation.3 | async-start | bytes 6291456 | tf_op jit(solution)/shard_map/all_to_all | solution.py:63
  357.8 11.6 %slice-start = ((s8[5242880]{0:T(1024)(128)(4,1)}), s8[1048576]{0:T(1024)(128)(4,1)S(1)}, s32[]{:S(2)}) async-start(s8[5242880]{0:T(1024)(128)(4,1)} %bitcast.68), calls=%async_computation.9 | async-start | bytes 2097152
  357.8 88.1 %all-to-all-start.2 = ((bf16[16,80,2048]{2,1,0:T(8,128)(2,1)}), bf16[16,80,2048]{2,1,0:T(8,128)(2,1)}, u32[]{:S(2)}, u32[]{:S(2)}) async-start(bf16[16,80,2048]{2,1,0:T(8,128)(2,1)} %bitcast.72), calls=%async_computation.2 | async-start | bytes 10485760 | tf_op jit(solution)/shard_map/all_to_all | solution.py:73
  365.8 4.0 slice-start.1
  445.9 5.6 copy-start.3
  445.9 86.1 %all-to-all-start.4 = ((bf16[16,80,2048]{2,1,0:T(8,128)(2,1)}), bf16[16,80,2048]{2,1,0:T(8,128)(2,1)}, u32[]{:S(2)}, u32[]{:S(2)}) async-start(bf16[16,80,2048]{2,1,0:T(8,128)(2,1)} %bitcast.73), calls=%async_computation.4 | async-start | bytes 10485760 | tf_op jit(solution)/shard_map/all_to_all | solution.py:73
  544.7 34.2 %copy-start.1 = (bf16[256,2048]{1,0:T(8,128)(2,1)S(1)}, bf16[256,2048]{1,0:T(8,128)(2,1)}, u32[]{:S(2)}) copy-start(bf16[256,2048]{1,0:T(8,128)(2,1)} %param.5) | copy-start | bytes 3145732
Sparse Core Ops, SparseCore 0:
  9.4 30.3 all-gather.6
  41.5 30.5 all-gather.8
  73.8 65.4 all-gather.10
  140.7 66.2 all-gather.12
